TPU v7x, 128 devices: a whole 4x4x4 slice. The times are simulated.
128 devices in a mesh: grp: 4 (over y), dev: 32 (over z, x, core).
Axes of the slice: x: 4, y: 4, z: 4, core: 2. Of those that a mesh axis runs over, the one named last changes fastest.
Arguments:
- examples: float32 [8192, 32768], P(('grp', 'dev'))
- labels: int32 [8192], P(('grp', 'dev')), may hold values from 0 to 1, as said below
Outputs:
- consensus: float32 [32768], replicated
- local_weights: float32 [128, 32768], P(('grp', 'dev'))
- dual_vars: float32 [128, 32768], P(('grp', 'dev'))
Inputs may be any that keep to these rules, and one draw needn't show every extreme that they name: `labels`: each example's class, 0 or 1.
All inputs are finite; a program needn't handle non-finite values.
Results may differ from a plain program's by a relative error of at most 0.00012.
Values sent between devices are 32-bit elements; how exact they have to be, the bound alone decides.
A program may use at most 64 MiB of HBM per device.

v0:
```python
import jax
import jax.numpy as jnp
from jax import lax
from jax.sharding import Mesh
from jax.sharding import PartitionSpec as P

PROX = 3
ROUNDS = 4
DEV = ("dev_0", "dev_1", "dev_2")
GRP_DEV = ("grp", "dev_0", "dev_1", "dev_2")


step_size = 200.0
penalty = 0.005
thresh = 0.04


def rows_for(lines, devices):
    spare = -lines.shape[0] % devices
    if not spare:
        return lines
    return jnp.concatenate([lines, jnp.zeros((spare, *lines.shape[1:]), lines.dtype)])


def from_everyone(x, axis):
    devices = lax.axis_size(axis)
    return lax.all_to_all(jnp.broadcast_to(x[None], (devices, *x.shape)), axis, 0, 0, tiled=True)


def laid_out(parts, dim):
    parts = jnp.moveaxis(parts, 0, dim)
    shape = parts.shape
    return parts.reshape(*shape[:dim], shape[dim] * shape[dim + 1], *shape[dim + 2 :])


def whole_of(x, axes, dim):
    far, near = axes
    initial = from_everyone(x, far)
    parts = jnp.swapaxes(from_everyone(initial, near), 0, 1)
    return laid_out(parts.reshape(-1, *x.shape), dim)


def cut_along(x, dim, devices):
    before, after = (x.shape[:dim], x.shape[dim + 1 :])
    return jnp.moveaxis(x.reshape(*before, devices, -1, *after), dim, 0)


def sent_and_summed(x, axis, dim):
    devices = lax.axis_size(axis)
    parts = lax.all_to_all(cut_along(x, dim, devices), axis, 0, 0, tiled=True)
    return jnp.sum(parts, axis=0)


def sum_in_two_steps(x, axes, dim):
    far, near = axes
    own = sent_and_summed(cut_along(x, dim, lax.axis_size(far)), near, dim + 1)
    return jnp.sum(lax.all_to_all(own, far, 0, 0, tiled=True), axis=0)


def sum_by_parts(x, axes):
    lines = x.reshape(-1)
    padded = rows_for(lines, lax.axis_size(axes[0]) * lax.axis_size(axes[1]))
    whole = whole_of(sum_in_two_steps(padded, axes, 0), axes, 0)
    return lax.slice_in_dim(whole, 0, len(lines)).reshape(x.shape)


def shrink(values):
    return values - jnp.clip(values, -thresh, thresh)


def local_steps(examples, targets, weight_vector, consensus_point):
    for prox_index in range(PROX):
        label_margins = jnp.dot(examples, weight_vector, precision=lax.Precision.HIGHEST)
        primal_residual = jax.nn.sigmoid(label_margins) - targets
        loss_gradient = jnp.dot(primal_residual, examples, precision=lax.Precision.HIGHEST)
        weight_vector = (
            weight_vector - step_size * loss_gradient + step_size * penalty * consensus_point
        ) / (1.0 + step_size * penalty)
    return weight_vector


def per_device(examples, labels):
    members = lax.axis_size("grp") * lax.axis_size(DEV)
    targets = labels.astype(jnp.float32)
    width = examples.shape[1]

    def one_round(round_index, carried):
        consensus, weight_vector, dual_vars = carried
        consensus_point = consensus - dual_vars
        weight_vector = local_steps(examples, targets, weight_vector, consensus_point)
        combined = weight_vector + dual_vars
        summed = sum_by_parts(combined, (("grp", "dev_0", "dev_1"), "dev_2"))
        consensus = shrink(summed / members)
        dual_vars = dual_vars + weight_vector - consensus
        return (consensus, weight_vector, dual_vars)

    start = (
        jnp.zeros((width,), jnp.float32),
        jnp.zeros((width,), jnp.float32),
        jnp.zeros((width,), jnp.float32),
    )
    consensus, weight_vector, dual_vars = lax.fori_loop(0, ROUNDS, one_round, start)
    return (consensus, weight_vector[None, :], dual_vars[None, :])


def solution(mesh):
    torus = Mesh(
        mesh.devices.reshape(mesh.shape["grp"], 4, 4, 2), ("grp", "dev_0", "dev_1", "dev_2")
    )
    return jax.shard_map(
        per_device,
        mesh=torus,
        in_specs=(P(GRP_DEV, None), P(GRP_DEV)),
        out_specs=(P(), P(GRP_DEV, None), P(GRP_DEV, None)),
        check_vma=False,
    )
```

profile of v0, /device:TPU:1, one launch (start us, length us, event | category | flops | bytes accessed | tf_op | source)
XLA Modules:
  0.0 299.4 jit_solution(6876343154307500842)
XLA Ops:
  0.6 0.7 convert_element_type.3
  1.3 297.4 %while.15 = (s32[]{:T(128)}, f32[32768]{0:T(1024)S(1)}, f32[32768]{0:T(1024)S(1)}, f32[32768]{0:T(1024)S(1)}, f32[64,32768]{1,0:T(8,128)}, /*index=5*/f32[64]{0:T(128)S(1)}, s32[]{:T(128)}, s32[]{:T(128)}, f32[]{:T(128)}) while((s32[]{:T(128)}, f32[32768]{0:T(1024)S(1)}, f32[32768]{0:T(1024)S(1)}, f32[32768]{0:T(1024)S(1)}, ...), condition=%wide.region_3.4_spmd.clone, body=%wide.region_0.3_spmd.clone.sunk | while | flops 151781888 | bytes 90509728 | solution.py:102
  1.3 9.1 %fusion.65 = f32[64,1]{0,1:T(1,128)S(1)} fusion(f32[64]{0:T(128)S(1)} %get-tuple-element.151, f32[64,32768]{1,0:T(8,128)} %get-tuple-element.150, f32[32768,1]{0,1:T(1,128)S(1)} %bitcast.138), kind=kOutput, calls=%fused_computation.20.clone.1 | convolution fusion | flops 25166080 | bytes 8520192 | tf_op jit(solution)/shard_map/while/body/eval_jaxpr/dot_general | solution.py:73
  10.4 4.0 %fusion.66 = f32[1,32768]{1,0:T(1,128)S(1)} fusion(f32[64,1]{0,1:T(1,128)S(1)} %fusion.65, f32[64,32768]{1,0:T(8,128)S(1)} %copy-done), kind=kOutput, calls=%fused_computation.32.clone.1 | convolution fusion | flops 25165824 | bytes 8519936 | tf_op jit(solution)/shard_map/while/body/eval_jaxpr/dot_general | solution.py:75
  14.5 6.6 %fusion.67 = f32[64,1]{0,1:T(1,128)S(1)} fusion(f32[64]{0:T(128)S(1)} %get-tuple-element.151, f32[32768,1]{0,1:T(1,128)S(1)} %bitcast.137, f32[64,32768]{1,0:T(8,128)S(1)} %copy-done), kind=kOutput, calls=%fused_computation.13.clone.1 | convolution fusion | flops 25166080 | bytes 8520192 | tf_op jit(solution)/shard_map/while/body/eval_jaxpr/dot_general | solution.py:73
  21.1 4.1 %fusion.68 = f32[1,32768]{1,0:T(1,128)S(1)} fusion(f32[64,1]{0,1:T(1,128)S(1)} %fusion.67, f32[64,32768]{1,0:T(8,128)S(1)} %copy-done), kind=kOutput, calls=%fused_computation.33.clone.1 | convolution fusion | flops 25165824 | bytes 8519936 | tf_op jit(solution)/shard_map/while/body/eval_jaxpr/dot_general | solution.py:75
  25.1 6.6 %fusion.69 = f32[64,1]{0,1:T(1,128)S(1)} fusion(f32[64]{0:T(128)S(1)} %get-tuple-element.151, f32[32768,1]{0,1:T(1,128)S(1)} %bitcast.136, f32[64,32768]{1,0:T(8,128)S(1)} %copy-done), kind=kOutput, calls=%fused_computation.6.clone.1 | convolution fusion | flops 25166080 | bytes 8520192 | tf_op jit(solution)/shard_map/while/body/eval_jaxpr/dot_general | solution.py:73
  31.7 4.1 %fusion.70 = f32[1,32768]{1,0:T(1,128)S(1)} fusion(f32[64,1]{0,1:T(1,128)S(1)} %fusion.69, f32[64,32768]{1,0:T(8,128)S(1)} %copy-done), kind=kOutput, calls=%fused_computation.34.clone.1 | convolution fusion | flops 25165824 | bytes 8519936 | tf_op jit(solution)/shard_map/while/body/eval_jaxpr/dot_general | solution.py:75
  35.8 0.1 reshape.36
  35.9 4.9 %all_to_all.35 = f32[2,64,256]{2,1,0:T(8,128)S(1)} all-to-all(f32[2,64,256]{2,1,0:T(8,128)S(1)} %copy.18), channel_id=1, replica_groups=mesh['grp'=4,'dev_0'=4,'dev_1'=4,'dev_2'=2] {'dev_2'}, dimensions={0} | all-to-all | bytes 262144 | tf_op jit(solution)/shard_map/while/body/eval_jaxpr/all_to_all | solution.py:50
  40.9 19.6 %all_to_all.36 = f32[64,1,256]{2,1,0:T(1,128)S(1)} all-to-all(f32[64,1,256]{2,1,0:T(1,128)S(1)} %all_to_all.27), channel_id=1, replica_groups=mesh['grp'=4,'dev_0'=4,'dev_1'=4,'dev_2'=2] {'grp','dev_0','dev_1'}, dimensions={0} | all-to-all | bytes 131072 | tf_op jit(solution)/shard_map/while/body/eval_jaxpr/all_to_all | solution.py:57
  60.5 0.1 reduce_sum.23
  60.6 0.7 broadcast_in_dim.27
  61.2 5.0 %all-to-all-start.2 = ((f32[64,1,256]{2,1,0:T(1,128)}), f32[64,1,256]{2,1,0:T(1,128)S(1)}, u32[]{:S(2)}, u32[]{:S(2)}) async-start(f32[64,1,256]{2,1,0:T(1,128)} %broadcast_in_dim.27), calls=%async_computation.2 | async-start | bytes 131072 | tf_op jit(solution)/shard_map/while/body/eval_jaxpr/all_to_all | solution.py:27
  66.2 8.4 %all-to-all-done.2 = f32[64,1,256]{2,1,0:T(1,128)S(1)} async-done(((f32[64,1,256]{2,1,0:T(1,128)}), f32[64,1,256]{2,1,0:T(1,128)S(1)}, u32[]{:S(2)}, u32[]{:S(2)}) %all-to-all-start.2) | async-done | bytes 65568 | tf_op jit(solution)/shard_map/while/body/eval_jaxpr/all_to_all | solution.py:27
  74.7 6.4 %all_to_all.37 = f32[2,64,256]{2,1,0:T(8,128)S(1)} all-to-all(f32[2,64,256]{2,1,0:T(8,128)S(1)} %broadcast_in_dim.28), channel_id=1, replica_groups=mesh['grp'=4,'dev_0'=4,'dev_1'=4,'dev_2'=2] {'dev_2'}, dimensions={0} | all-to-all | bytes 262144 | tf_op jit(solution)/shard_map/while/body/eval_jaxpr/all_to_all | solution.py:27
  81.1 0.1 copy.20
  81.4 9.1 %fusion.65 = f32[64,1]{0,1:T(1,128)S(1)} fusion(f32[64]{0:T(128)S(1)} %get-tuple-element.151, f32[64,32768]{1,0:T(8,128)} %get-tuple-element.150, f32[32768,1]{0,1:T(1,128)S(1)} %bitcast.138), kind=kOutput, calls=%fused_computation.20.clone.1 | convolution fusion | flops 25166080 | bytes 8520192 | tf_op jit(solution)/shard_map/while/body/eval_jaxpr/dot_general | solution.py:73
  90.4 4.0 %fusion.66 = f32[1,32768]{1,0:T(1,128)S(1)} fusion(f32[64,1]{0,1:T(1,128)S(1)} %fusion.65, f32[64,32768]{1,0:T(8,128)S(1)} %copy-done), kind=kOutput, calls=%fused_computation.32.clone.1 | convolution fusion | flops 25165824 | bytes 8519936 | tf_op jit(solution)/shard_map/while/body/eval_jaxpr/dot_general | solution.py:75
  94.5 6.6 %fusion.67 = f32[64,1]{0,1:T(1,128)S(1)} fusion(f32[64]{0:T(128)S(1)} %get-tuple-element.151, f32[32768,1]{0,1:T(1,128)S(1)} %bitcast.137, f32[64,32768]{1,0:T(8,128)S(1)} %copy-done), kind=kOutput, calls=%fused_computation.13.clone.1 | convolution fusion | flops 25166080 | bytes 8520192 | tf_op jit(solution)/shard_map/while/body/eval_jaxpr/dot_general | solution.py:73
  101.1 4.1 %fusion.68 = f32[1,32768]{1,0:T(1,128)S(1)} fusion(f32[64,1]{0,1:T(1,128)S(1)} %fusion.67, f32[64,32768]{1,0:T(8,128)S(1)} %copy-done), kind=kOutput, calls=%fused_computation.33.clone.1 | convolution fusion | flops 25165824 | bytes 8519936 | tf_op jit(solution)/shard_map/while/body/eval_jaxpr/dot_general | solution.py:75
  105.2 6.6 %fusion.69 = f32[64,1]{0,1:T(1,128)S(1)} fusion(f32[64]{0:T(128)S(1)} %get-tuple-element.151, f32[32768,1]{0,1:T(1,128)S(1)} %bitcast.136, f32[64,32768]{1,0:T(8,128)S(1)} %copy-done), kind=kOutput, calls=%fused_computation.6.clone.1 | convolution fusion | flops 25166080 | bytes 8520192 | tf_op jit(solution)/shard_map/while/body/eval_jaxpr/dot_general | solution.py:73
  111.8 4.1 %fusion.70 = f32[1,32768]{1,0:T(1,128)S(1)} fusion(f32[64,1]{0,1:T(1,128)S(1)} %fusion.69, f32[64,32768]{1,0:T(8,128)S(1)} %copy-done), kind=kOutput, calls=%fused_computation.34.clone.1 | convolution fusion | flops 25165824 | bytes 8519936 | tf_op jit(solution)/shard_map/while/body/eval_jaxpr/dot_general | solution.py:75
  115.9 0.1 reshape.36
  116.0 3.8 %all_to_all.35 = f32[2,64,256]{2,1,0:T(8,128)S(1)} all-to-all(f32[2,64,256]{2,1,0:T(8,128)S(1)} %copy.18), channel_id=1, replica_groups=mesh['grp'=4,'dev_0'=4,'dev_1'=4,'dev_2'=2] {'dev_2'}, dimensions={0} | all-to-all | bytes 262144 | tf_op jit(solution)/shard_map/while/body/eval_jaxpr/all_to_all | solution.py:50
  119.9 13.0 %all_to_all.36 = f32[64,1,256]{2,1,0:T(1,128)S(1)} all-to-all(f32[64,1,256]{2,1,0:T(1,128)S(1)} %all_to_all.27), channel_id=1, replica_groups=mesh['grp'=4,'dev_0'=4,'dev_1'=4,'dev_2'=2] {'grp','dev_0','dev_1'}, dimensions={0} | all-to-all | bytes 131072 | tf_op jit(solution)/shard_map/while/body/eval_jaxpr/all_to_all | solution.py:57
  132.9 0.1 reduce_sum.23
  133.0 0.7 broadcast_in_dim.27
  133.7 5.0 %all-to-all-start.2 = ((f32[64,1,256]{2,1,0:T(1,128)}), f32[64,1,256]{2,1,0:T(1,128)S(1)}, u32[]{:S(2)}, u32[]{:S(2)}) async-start(f32[64,1,256]{2,1,0:T(1,128)} %broadcast_in_dim.27), calls=%async_computation.2 | async-start | bytes 131072 | tf_op jit(solution)/shard_map/while/body/eval_jaxpr/all_to_all | solution.py:27
  138.7 8.4 %all-to-all-done.2 = f32[64,1,256]{2,1,0:T(1,128)S(1)} async-done(((f32[64,1,256]{2,1,0:T(1,128)}), f32[64,1,256]{2,1,0:T(1,128)S(1)}, u32[]{:S(2)}, u32[]{:S(2)}) %all-to-all-start.2) | async-done | bytes 65568 | tf_op jit(solution)/shard_map/while/body/eval_jaxpr/all_to_all | solution.py:27
  147.1 6.4 %all_to_all.37 = f32[2,64,256]{2,1,0:T(8,128)S(1)} all-to-all(f32[2,64,256]{2,1,0:T(8,128)S(1)} %broadcast_in_dim.28), channel_id=1, replica_groups=mesh['grp'=4,'dev_0'=4,'dev_1'=4,'dev_2'=2] {'dev_2'}, dimensions={0} | all-to-all | bytes 262144 | tf_op jit(solution)/shard_map/while/body/eval_jaxpr/all_to_all | solution.py:27
  153.5 0.1 copy.20
  153.8 9.1 %fusion.65 = f32[64,1]{0,1:T(1,128)S(1)} fusion(f32[64]{0:T(128)S(1)} %get-tuple-element.151, f32[64,32768]{1,0:T(8,128)} %get-tuple-element.150, f32[32768,1]{0,1:T(1,128)S(1)} %bitcast.138), kind=kOutput, calls=%fused_computation.20.clone.1 | convolution fusion | flops 25166080 | bytes 8520192 | tf_op jit(solution)/shard_map/while/body/eval_jaxpr/dot_general | solution.py:73
  162.9 4.0 %fusion.66 = f32[1,32768]{1,0:T(1,128)S(1)} fusion(f32[64,1]{0,1:T(1,128)S(1)} %fusion.65, f32[64,32768]{1,0:T(8,128)S(1)} %copy-done), kind=kOutput, calls=%fused_computation.32.clone.1 | convolution fusion | flops 25165824 | bytes 8519936 | tf_op jit(solution)/shard_map/while/body/eval_jaxpr/dot_general | solution.py:75
  167.0 6.6 %fusion.67 = f32[64,1]{0,1:T(1,128)S(1)} fusion(f32[64]{0:T(128)S(1)} %get-tuple-element.151, f32[32768,1]{0,1:T(1,128)S(1)} %bitcast.137, f32[64,32768]{1,0:T(8,128)S(1)} %copy-done), kind=kOutput, calls=%fused_computation.13.clone.1 | convolution fusion | flops 25166080 | bytes 8520192 | tf_op jit(solution)/shard_map/while/body/eval_jaxpr/dot_general | solution.py:73
  173.5 4.1 %fusion.68 = f32[1,32768]{1,0:T(1,128)S(1)} fusion(f32[64,1]{0,1:T(1,128)S(1)} %fusion.67, f32[64,32768]{1,0:T(8,128)S(1)} %copy-done), kind=kOutput, calls=%fused_computation.33.clone.1 | convolution fusion | flops 25165824 | bytes 8519936 | tf_op jit(solution)/shard_map/while/body/eval_jaxpr/dot_general | solution.py:75
  177.6 6.6 %fusion.69 = f32[64,1]{0,1:T(1,128)S(1)} fusion(f32[64]{0:T(128)S(1)} %get-tuple-element.151, f32[32768,1]{0,1:T(1,128)S(1)} %bitcast.136, f32[64,32768]{1,0:T(8,128)S(1)} %copy-done), kind=kOutput, calls=%fused_computation.6.clone.1 | convolution fusion | flops 25166080 | bytes 8520192 | tf_op jit(solution)/shard_map/while/body/eval_jaxpr/dot_general | solution.py:73
  184.2 4.1 %fusion.70 = f32[1,32768]{1,0:T(1,128)S(1)} fusion(f32[64,1]{0,1:T(1,128)S(1)} %fusion.69, f32[64,32768]{1,0:T(8,128)S(1)} %copy-done), kind=kOutput, calls=%fused_computation.34.clone.1 | convolution fusion | flops 25165824 | bytes 8519936 | tf_op jit(solution)/shard_map/while/body/eval_jaxpr/dot_general | solution.py:75
  188.3 0.1 reshape.36
  188.4 3.8 %all_to_all.35 = f32[2,64,256]{2,1,0:T(8,128)S(1)} all-to-all(f32[2,64,256]{2,1,0:T(8,128)S(1)} %copy.18), channel_id=1, replica_groups=mesh['grp'=4,'dev_0'=4,'dev_1'=4,'dev_2'=2] {'dev_2'}, dimensions={0} | all-to-all | bytes 262144 | tf_op jit(solution)/shard_map/while/body/eval_jaxpr/all_to_all | solution.py:50
  192.3 13.0 %all_to_all.36 = f32[64,1,256]{2,1,0:T(1,128)S(1)} all-to-all(f32[64,1,256]{2,1,0:T(1,128)S(1)} %all_to_all.27), channel_id=1, replica_groups=mesh['grp'=4,'dev_0'=4,'dev_1'=4,'dev_2'=2] {'grp','dev_0','dev_1'}, dimensions={0} | all-to-all | bytes 131072 | tf_op jit(solution)/shard_map/while/body/eval_jaxpr/all_to_all | solution.py:57
  205.4 0.1 reduce_sum.23
  205.5 0.7 broadcast_in_dim.27
  206.1 5.0 %all-to-all-start.2 = ((f32[64,1,256]{2,1,0:T(1,128)}), f32[64,1,256]{2,1,0:T(1,128)S(1)}, u32[]{:S(2)}, u32[]{:S(2)}) async-start(f32[64,1,256]{2,1,0:T(1,128)} %broadcast_in_dim.27), calls=%async_computation.2 | async-start | bytes 131072 | tf_op jit(solution)/shard_map/while/body/eval_jaxpr/all_to_all | solution.py:27
  211.1 8.4 %all-to-all-done.2 = f32[64,1,256]{2,1,0:T(1,128)S(1)} async-done(((f32[64,1,256]{2,1,0:T(1,128)}), f32[64,1,256]{2,1,0:T(1,128)S(1)}, u32[]{:S(2)}, u32[]{:S(2)}) %all-to-all-start.2) | async-done | bytes 65568 | tf_op jit(solution)/shard_map/while/body/eval_jaxpr/all_to_all | solution.py:27
  219.6 6.4 %all_to_all.37 = f32[2,64,256]{2,1,0:T(8,128)S(1)} all-to-all(f32[2,64,256]{2,1,0:T(8,128)S(1)} %broadcast_in_dim.28), channel_id=1, replica_groups=mesh['grp'=4,'dev_0'=4,'dev_1'=4,'dev_2'=2] {'dev_2'}, dimensions={0} | all-to-all | bytes 262144 | tf_op jit(solution)/shard_map/while/body/eval_jaxpr/all_to_all | solution.py:27
  226.0 0.1 copy.20
  226.1 0.1 copy.21
  226.3 9.1 %fusion.65 = f32[64,1]{0,1:T(1,128)S(1)} fusion(f32[64]{0:T(128)S(1)} %get-tuple-element.151, f32[64,32768]{1,0:T(8,128)} %get-tuple-element.150, f32[32768,1]{0,1:T(1,128)S(1)} %bitcast.138), kind=kOutput, calls=%fused_computation.20.clone.1 | convolution fusion | flops 25166080 | bytes 8520192 | tf_op jit(solution)/shard_map/while/body/eval_jaxpr/dot_general | solution.py:73
  235.3 4.0 %fusion.66 = f32[1,32768]{1,0:T(1,128)S(1)} fusion(f32[64,1]{0,1:T(1,128)S(1)} %fusion.65, f32[64,32768]{1,0:T(8,128)S(1)} %copy-done), kind=kOutput, calls=%fused_computation.32.clone.1 | convolution fusion | flops 25165824 | bytes 8519936 | tf_op jit(solution)/shard_map/while/body/eval_jaxpr/dot_general | solution.py:75
  239.4 6.6 %fusion.67 = f32[64,1]{0,1:T(1,128)S(1)} fusion(f32[64]{0:T(128)S(1)} %get-tuple-element.151, f32[32768,1]{0,1:T(1,128)S(1)} %bitcast.137, f32[64,32768]{1,0:T(8,128)S(1)} %copy-done), kind=kOutput, calls=%fused_computation.13.clone.1 | convolution fusion | flops 25166080 | bytes 8520192 | tf_op jit(solution)/shard_map/while/body/eval_jaxpr/dot_general | solution.py:73
  246.0 4.1 %fusion.68 = f32[1,32768]{1,0:T(1,128)S(1)} fusion(f32[64,1]{0,1:T(1,128)S(1)} %fusion.67, f32[64,32768]{1,0:T(8,128)S(1)} %copy-done), kind=kOutput, calls=%fused_computation.33.clone.1 | convolution fusion | flops 25165824 | bytes 8519936 | tf_op jit(solution)/shard_map/while/body/eval_jaxpr/dot_general | solution.py:75
  250.1 6.6 %fusion.69 = f32[64,1]{0,1:T(1,128)S(1)} fusion(f32[64]{0:T(128)S(1)} %get-tuple-element.151, f32[32768,1]{0,1:T(1,128)S(1)} %bitcast.136, f32[64,32768]{1,0:T(8,128)S(1)} %copy-done), kind=kOutput, calls=%fused_computation.6.clone.1 | convolution fusion | flops 25166080 | bytes 8520192 | tf_op jit(solution)/shard_map/while/body/eval_jaxpr/dot_general | solution.py:73
  256.7 4.1 %fusion.70 = f32[1,32768]{1,0:T(1,128)S(1)} fusion(f32[64,1]{0,1:T(1,128)S(1)} %fusion.69, f32[64,32768]{1,0:T(8,128)S(1)} %copy-done), kind=kOutput, calls=%fused_computation.34.clone.1 | convolution fusion | flops 25165824 | bytes 8519936 | tf_op jit(solution)/shard_map/while/body/eval_jaxpr/dot_general | solution.py:75
  260.8 0.1 reshape.36
  260.9 3.8 %all_to_all.35 = f32[2,64,256]{2,1,0:T(8,128)S(1)} all-to-all(f32[2,64,256]{2,1,0:T(8,128)S(1)} %copy.18), channel_id=1, replica_groups=mesh['grp'=4,'dev_0'=4,'dev_1'=4,'dev_2'=2] {'dev_2'}, dimensions={0} | all-to-all | bytes 262144 | tf_op jit(solution)/shard_map/while/body/eval_jaxpr/all_to_all | solution.py:50
  264.8 13.0 %all_to_all.36 = f32[64,1,256]{2,1,0:T(1,128)S(1)} all-to-all(f32[64,1,256]{2,1,0:T(1,128)S(1)} %all_to_all.27), channel_id=1, replica_groups=mesh['grp'=4,'dev_0'=4,'dev_1'=4,'dev_2'=2] {'grp','dev_0','dev_1'}, dimensions={0} | all-to-all | bytes 131072 | tf_op jit(solution)/shard_map/while/body/eval_jaxpr/all_to_all | solution.py:57
  277.8 0.1 reduce_sum.23
  277.9 0.7 broadcast_in_dim.27
  278.6 5.0 %all-to-all-start.2 = ((f32[64,1,256]{2,1,0:T(1,128)}), f32[64,1,256]{2,1,0:T(1,128)S(1)}, u32[]{:S(2)}, u32[]{:S(2)}) async-start(f32[64,1,256]{2,1,0:T(1,128)} %broadcast_in_dim.27), calls=%async_computation.2 | async-start | bytes 131072 | tf_op jit(solution)/shard_map/while/body/eval_jaxpr/all_to_all | solution.py:27
  283.6 8.4 %all-to-all-done.2 = f32[64,1,256]{2,1,0:T(1,128)S(1)} async-done(((f32[64,1,256]{2,1,0:T(1,128)}), f32[64,1,256]{2,1,0:T(1,128)S(1)}, u32[]{:S(2)}, u32[]{:S(2)}) %all-to-all-start.2) | async-done | bytes 65568 | tf_op jit(solution)/shard_map/while/body/eval_jaxpr/all_to_all | solution.py:27
  292.0 6.4 %all_to_all.37 = f32[2,64,256]{2,1,0:T(8,128)S(1)} all-to-all(f32[2,64,256]{2,1,0:T(8,128)S(1)} %broadcast_in_dim.28), channel_id=1, replica_groups=mesh['grp'=4,'dev_0'=4,'dev_1'=4,'dev_2'=2] {'dev_2'}, dimensions={0} | all-to-all | bytes 262144 | tf_op jit(solution)/shard_map/while/body/eval_jaxpr/all_to_all | solution.py:27
  298.4 0.1 copy.20
  298.7 0.6 copy-done.1
  (63 shorter events, 1.3 us)
Async XLA Ops:
  1.3 9.1 %copy-start = (f32[64,32768]{1,0:T(8,128)S(1)}, f32[64,32768]{1,0:T(8,128)}, u32[]{:S(2)}) copy-start(f32[64,32768]{1,0:T(8,128)} %get-tuple-element.150) | copy-start | bytes 25165828 | tf_op jit(solution)/shard_map/while
  61.2 13.4 %all-to-all-start.2 = ((f32[64,1,256]{2,1,0:T(1,128)}), f32[64,1,256]{2,1,0:T(1,128)S(1)}, u32[]{:S(2)}, u32[]{:S(2)}) async-start(f32[64,1,256]{2,1,0:T(1,128)} %broadcast_in_dim.27), calls=%async_computation.2 | async-start | bytes 131072 | tf_op jit(solution)/shard_map/while/body/eval_jaxpr/all_to_all | solution.py:27
  81.3 9.1 %copy-start = (f32[64,32768]{1,0:T(8,128)S(1)}, f32[64,32768]{1,0:T(8,128)}, u32[]{:S(2)}) copy-start(f32[64,32768]{1,0:T(8,128)} %get-tuple-element.150) | copy-start | bytes 25165828 | tf_op jit(solution)/shard_map/while
  133.7 13.4 %all-to-all-start.2 = ((f32[64,1,256]{2,1,0:T(1,128)}), f32[64,1,256]{2,1,0:T(1,128)S(1)}, u32[]{:S(2)}, u32[]{:S(2)}) async-start(f32[64,1,256]{2,1,0:T(1,128)} %broadcast_in_dim.27), calls=%async_computation.2 | async-start | bytes 131072 | tf_op jit(solution)/shard_map/while/body/eval_jaxpr/all_to_all | solution.py:27
  153.8 9.1 %copy-start = (f32[64,32768]{1,0:T(8,128)S(1)}, f32[64,32768]{1,0:T(8,128)}, u32[]{:S(2)}) copy-start(f32[64,32768]{1,0:T(8,128)} %get-tuple-element.150) | copy-start | bytes 25165828 | tf_op jit(solution)/shard_map/while
  206.1 13.4 %all-to-all-start.2 = ((f32[64,1,256]{2,1,0:T(1,128)}), f32[64,1,256]{2,1,0:T(1,128)S(1)}, u32[]{:S(2)}, u32[]{:S(2)}) async-start(f32[64,1,256]{2,1,0:T(1,128)} %broadcast_in_dim.27), calls=%async_computation.2 | async-start | bytes 131072 | tf_op jit(solution)/shard_map/while/body/eval_jaxpr/all_to_all | solution.py:27
  226.2 9.1 %copy-start = (f32[64,32768]{1,0:T(8,128)S(1)}, f32[64,32768]{1,0:T(8,128)}, u32[]{:S(2)}) copy-start(f32[64,32768]{1,0:T(8,128)} %get-tuple-element.150) | copy-start | bytes 25165828 | tf_op jit(solution)/shard_map/while
  278.6 13.4 %all-to-all-start.2 = ((f32[64,1,256]{2,1,0:T(1,128)}), f32[64,1,256]{2,1,0:T(1,128)S(1)}, u32[]{:S(2)}, u32[]{:S(2)}) async-start(f32[64,1,256]{2,1,0:T(1,128)} %broadcast_in_dim.27), calls=%async_computation.2 | async-start | bytes 131072 | tf_op jit(solution)/shard_map/while/body/eval_jaxpr/all_to_all | solution.py:27
  298.7 0.7 copy-start.1
  298.7 0.7 copy-start.2
  298.7 0.7 copy-start.3
where the time goes:
time: 300 us; the launch traced here: 299 us
  matrix products  137 us (46%)
  blocking collectives  101 us (34%)
  waiting for transfers between devices  33.7 us (11%)
  starting transfers between devices  19.9 us (7%)
  local copies, waits for them, and re-layouts  4.75 us (2%)
    dot_general x12, matrix products, local_steps(): jnp.dot(examples, weight_vector, precision=lax.Precision.HIGHEST)  88.9 us
    all_to_all x4, blocking collectives, sum_in_two_steps(): return jnp.sum(lax.all_to_all(own, far, 0, 0, tiled=True), axis=0)  58.7 us
    dot_general x12, matrix products, local_steps(): jnp.dot(primal_residual, examples, precision=lax.Precision.HIGHEST)  48.6 us
    all_to_all x4, waiting for transfers between devices, from_everyone(): lax.all_to_all(jnp.broadcast_to(x[None], (devices, *x.shape)), axis, 0, 0...  33.7 us
    all_to_all x4, blocking collectives, from_everyone(): lax.all_to_all(jnp.broadcast_to(x[None], (devices, *x.shape)), axis, 0, 0...  25.6 us
    all_to_all x4, starting transfers between devices, from_everyone(): lax.all_to_all(jnp.broadcast_to(x[None], (devices, *x.shape)), axis, 0, 0...  19.9 us
    all_to_all x4, blocking collectives, sent_and_summed(): parts = lax.all_to_all(cut_along(x, dim, devices), axis, 0, 0, tiled=True)  16.4 us
  transfers between devices with their start and end apart: 4, of which 4 were waited for; matrix products, arithmetic and copies ran while one was open for 0% of the time, Pallas kernels for 0%

commit v1 on v0

v1 whole, which is shorter than its diff:
```python
import jax
import jax.numpy as jnp
from jax import lax
from jax.experimental import pallas as pl
from jax.experimental.pallas import tpu as pltpu
from jax.sharding import PartitionSpec as P

PROX = 3
ROUNDS = 4
THRESH = 0.04
STEP = 200.0
PENALTY = 0.005
MESH = pl.DeviceIdType.MESH
CHUNKS = 8
BF16 = jnp.bfloat16
F32 = jnp.float32

ORDER = (2, 1, 3, 0)
PEERS = sorted(
    [
        (dy, dz, dx, dc)
        for dy in ORDER
        for dz in ORDER
        for dx in ORDER
        for dc in (1, 0)
        if (dy, dz, dx, dc) != (0, 0, 0, 0)
    ],
    key=lambda o: -sum(min(d, 4 - d) for d in o[:3]),
)


def kernel(rows, feats, n, labels_ref, x_hbm, z_ref, w_ref, u_ref, xv, gram, h, rs, zb, zmine, x_sems, send_rs, recv_rs, send_ag, recv_ag):
    grp = lax.axis_index("grp")
    dev = lax.axis_index("dev")
    me = grp * 32 + dev
    core = lax.rem(dev, 2)
    px = lax.rem(lax.div(dev, 2), 4)
    pz = lax.div(dev, 8)
    width = feats // CHUNKS

    def copy_in(c):
        cols = pl.ds(c * width, width)
        return pltpu.make_async_copy(x_hbm.at[:, cols], xv.at[:, cols], x_sems.at[c])

    for c in range(CHUNKS):
        copy_in(c).start()

    ys = [lax.rem(grp + d, 4) for d in range(4)]
    zs = [lax.rem(pz + d, 4) * 8 for d in range(4)]
    xs = [lax.rem(px + d, 4) * 2 for d in range(4)]
    cs = [core, 1 - core]

    def peer(offset):
        dy, dz, dx, dc = offset
        ty = ys[dy]
        td = zs[dz] + xs[dx] + cs[dc]
        return ty, td

    barrier = pltpu.get_barrier_semaphore()
    for offset in PEERS:
        pl.semaphore_signal(barrier, inc=1, device_id=peer(offset), device_id_type=MESH)

    sub = 512
    acc = jnp.zeros((2 * rows, rows), F32)
    for c in range(CHUNKS):
        copy_in(c).wait()

        def gram_step(i, acc, c=c):
            xs_ = xv[:, pl.ds(pl.multiple_of(c * width + i * sub, sub), sub)]
            hi = xs_.astype(BF16)
            lo = (xs_ - hi.astype(F32)).astype(BF16)
            both = jnp.concatenate([hi, lo], axis=0)
            return acc + lax.dot_general(both, hi, (((1,), (1,)), ((), ())), preferred_element_type=F32)

        acc = lax.fori_loop(0, width // sub, gram_step, acc)
    cross = acc[rows:]
    gram[...] = acc[:rows] + cross + cross.T

    r_i = lax.broadcasted_iota(jnp.int32, (rows, rows), 0)
    c_i = lax.broadcasted_iota(jnp.int32, (rows, rows), 1)
    eye = r_i == c_i
    targets = jnp.sum(jnp.where(eye, labels_ref[...].astype(F32), 0.0), axis=1, keepdims=True)

    w_ref[...] = jnp.zeros_like(w_ref)
    u_ref[...] = jnp.zeros_like(u_ref)
    zb[...] = jnp.zeros_like(zb)

    pl.semaphore_wait(barrier, n - 1)

    def gram_times(r):
        r_row = jnp.sum(jnp.where(eye, r, 0.0), axis=0, keepdims=True)
        return jnp.sum(gram[...] * r_row, axis=1, keepdims=True)

    def one_round(k, carried):
        m, xu, xz, mean_w, mean_u, z_own = carried
        par = lax.rem(k, 2)
        prev = 1 - par
        q = xz - xu
        total = jnp.zeros((rows, 1), F32)
        for t in range(PROX):
            r = jax.nn.sigmoid(m) - targets
            total = 0.5 * total + r
            m = 0.5 * (m + q) - (STEP * 0.5) * gram_times(r)
        scaled = jnp.broadcast_to((-STEP * 0.5) * total, (rows, 128))

        def back(j, _):
            for half in range(2):
                cols = pl.ds(pl.multiple_of(j * 256 + half * 128, 128), 128)
                h[j, half : half + 1, :] = jnp.sum(xv[:, cols] * scaled, axis=0, keepdims=True)
            return 0

        lax.fori_loop(0, n, back, 0, unroll=4)

        for offset in PEERS:
            ty, td = peer(offset)
            pltpu.make_async_remote_copy(
                src_ref=h.at[ty * 32 + td],
                dst_ref=rs.at[me],
                send_sem=send_rs,
                recv_sem=recv_rs,
                device_id=(ty, td),
                device_id_type=MESH,
            ).start()
        rs[me] = h[me]
        u = u_ref[...] + jnp.where(k > 0, 1.0, 0.0) * (w_ref[...] - zb[prev])
        u_ref[...] = u
        w_ref[...] = 0.125 * w_ref[...] + 0.875 * (zb[prev] - u) + h[...]

        some = rs.at[pl.ds(0, n - 1)]
        waiter = pltpu.make_async_remote_copy(
            src_ref=some, dst_ref=some, send_sem=send_rs, recv_sem=recv_rs, device_id=(grp, dev), device_id_type=MESH
        )
        waiter.wait_recv()
        mean_h = jnp.sum(rs[...], axis=0) * (1.0 / n)
        new_mean_w = 0.125 * mean_w + 0.875 * (z_own - mean_u) + mean_h
        a = new_mean_w + mean_u
        z_new = a - jnp.clip(a, -THRESH, THRESH)
        zmine[...] = z_new
        for offset in PEERS:
            ty, td = peer(offset)
            pltpu.make_async_remote_copy(
                src_ref=zmine,
                dst_ref=zb.at[par, me],
                send_sem=send_ag,
                recv_sem=recv_ag,
                device_id=(ty, td),
                device_id_type=MESH,
            ).start()
        zb[par, me] = z_new
        waiter.wait_send()
        got = zb.at[par, pl.ds(0, n - 1)]
        waiter_ag = pltpu.make_async_remote_copy(
            src_ref=got, dst_ref=got, send_sem=send_ag, recv_sem=recv_ag, device_id=(grp, dev), device_id_type=MESH
        )
        waiter_ag.wait_recv()

        def fwd(j, acc):
            for half in range(2):
                cols = pl.ds(pl.multiple_of(j * 256 + half * 128, 128), 128)
                acc = acc + xv[:, cols] * zb[par, j, half : half + 1, :]
            return acc

        acc = lax.fori_loop(0, n, fwd, jnp.zeros((rows, 128), F32), unroll=4)
        new_xz = jnp.sum(acc, axis=1, keepdims=True)
        waiter_ag.wait_send()
        xu = xu + m - new_xz
        return m, xu, new_xz, new_mean_w, a - z_new, z_new

    col = jnp.zeros((rows, 1), F32)
    piece = jnp.zeros((2, 128), F32)
    lax.fori_loop(0, ROUNDS, one_round, (col, col, col, piece, piece, piece))
    last = (ROUNDS - 1) % 2
    z_ref[...] = zb[last]
    u_ref[...] = u_ref[...] + w_ref[...] - zb[last]


def solution(mesh):
    n = mesh.size

    def per_device(examples, labels):
        rows, feats = examples.shape
        import functools

        vec = jax.ShapeDtypeStruct((n, 2, 128), F32)
        vmem = pl.BlockSpec(memory_space=pltpu.VMEM)
        z, w, u = pl.pallas_call(
            functools.partial(kernel, rows, feats, n),
            out_shape=(vec, vec, vec),
            in_specs=[vmem, pl.BlockSpec(memory_space=pl.ANY)],
            out_specs=(vmem, vmem, vmem),
            scratch_shapes=[
                pltpu.VMEM((rows, feats), F32),
                pltpu.VMEM((rows, rows), F32),
                pltpu.VMEM((n, 2, 128), F32),
                pltpu.VMEM((n, 2, 128), F32),
                pltpu.VMEM((2, n, 2, 128), F32),
                pltpu.VMEM((2, 128), F32),
                pltpu.SemaphoreType.DMA((CHUNKS,)),
                pltpu.SemaphoreType.DMA,
                pltpu.SemaphoreType.DMA,
                pltpu.SemaphoreType.DMA,
                pltpu.SemaphoreType.DMA,
            ],
            compiler_params=pltpu.CompilerParams(collective_id=0, has_side_effects=True),
        )(labels.reshape(1, rows), examples)
        return z.reshape(feats), w.reshape(1, feats), u.reshape(1, feats)

    return jax.shard_map(
        per_device,
        mesh=mesh,
        in_specs=(P(("grp", "dev"), None), P(("grp", "dev"))),
        out_specs=(P(), P(("grp", "dev"), None), P(("grp", "dev"), None)),
        check_vma=False,
    )
```

time: 300 us -> 85 us (0.28)
  matrix products: 137 us -> 0 us
  blocking collectives: 101 us -> 0 us
  Pallas kernels: 0 us -> 79.5 us
  waiting for transfers between devices: 33.7 us -> 0 us
  starting transfers between devices: 19.9 us -> 0 us
    dot_general x24 -> x0, matrix products: 137 us -> none  [the longest x12 88.9 us: local_steps(): jnp.dot(examples, weight_vector, precision=lax.Precision.HIGHEST)]
    all_to_all x12 -> x0, blocking collectives: 101 us -> none  [the longest x4 58.7 us: sum_in_two_steps(): return jnp.sum(lax.all_to_all(own, far, 0, 0, tiled=True), axis=0)]
    pallas_call x0 -> x1, Pallas kernels: none -> 79.5 us  [per_device(): pl.pallas_call(functools.partial(kernel, rows, feats, n), out_shape=(vec,...]
    all_to_all x4 -> x0, waiting for transfers between devices: 33.7 us -> none  [from_everyone(): lax.all_to_all(jnp.broadcast_to(x[None], (devices, *x.shape)), axis, 0, 0...]
    all_to_all x4 -> x0, starting transfers between devices: 19.9 us -> none  [from_everyone(): lax.all_to_all(jnp.broadcast_to(x[None], (devices, *x.shape)), axis, 0, 0...]
    unnamed x6 -> x3, local copies, waits for them, and re-layouts: 0.72 us -> 4.7 us
  transfers between devices with their start and end apart: 4 -> 0, of which waited for: 4 -> 0; matrix products, arithmetic and copies ran while one was open for 0% -> 0% of each run, Pallas kernels for 0% -> 0%
where the time goes in v1:
time: 85 us; the launch traced here: 84.8 us
  Pallas kernels  79.5 us (94%)
  local copies, waits for them, and re-layouts  4.7 us (6%)
    pallas_call x1, Pallas kernels, per_device(): pl.pallas_call(functools.partial(kernel, rows, feats, n), out_shape=(vec,...  79.5 us
    unnamed x3, local copies, waits for them, and re-layouts  4.7 us

profile of v1, /device:TPU:1, one launch (start us, length us, event | category | flops | bytes accessed | tf_op | source)
XLA Modules:
  0.0 84.8 jit_solution(8058001007781731043)
XLA Ops:
  0.6 79.5 %shard_map.49 = (f32[128,2,128]{2,1,0:T(2,128)}, f32[128,2,128]{2,1,0:T(2,128)}, f32[128,2,128]{2,1,0:T(2,128)}) custom-call(s32[1,64]{1,0:T(1,128)} %bitcast.7, f32[64,32768]{1,0:T(8,128)} %x_hbm.1), custom_call_target="tpu_custom_call" | custom-call | tf_op jit(solution)/shard_map/pallas_call | solution.py:186
  80.1 1.6 %copy.8 = f32[32768]{0:T(1024)} copy(f32[32768]{0:T(1024)} %bitcast.6) | data formatting | bytes 262144
  81.7 1.6 %copy.9 = f32[1,32768]{1,0:T(1,128)} copy(f32[1,32768]{1,0:T(1,128)} %bitcast.5) | data formatting | bytes 262144
  83.3 1.6 %copy.10 = f32[1,32768]{1,0:T(1,128)} copy(f32[1,32768]{1,0:T(1,128)} %bitcast.4) | data formatting | bytes 262144
